TPU v7x, 32 devices: a whole 2x2x4 slice. The times are simulated.
32 devices in a mesh: lat: 4 (over x, core), lon: 8 (over z, y).
Axes of the slice: x: 2, y: 2, z: 4, core: 2. Of those that a mesh axis runs over, the one named last changes fastest.
Arguments:
- tracers: bfloat16 [256, 1024, 32, 4], P('lat', 'lon'), may hold values from 0 to 2
- weights: bfloat16 [256, 8, 8, 128, 128], P('lat', 'lon'), may hold values from -1 to 1, as said below
- source_row: int32 [256, 8, 8], P('lat', 'lon'), may hold values from 0 to 255, as said below
- source_block: int32 [256, 8, 8], P('lat', 'lon'), may hold values from 0 to 7, as said below
- slot_count: int32 [256, 8], P('lat', 'lon'), may hold values from 1 to 8, as said below
Outputs:
- advected_fixed: float32 [256, 1024, 32, 4], P('lat', 'lon')
Inputs may be any that keep to these rules, and one draw needn't show every extreme that they name: source_row differs from the target tile's own row by at most 4 and lies within the grid. source_block lies at cyclic distance at most 2 from the target tile's own index along the row, except for target tiles of the first and the last latitude row, where it may reach 3; the allowed distance grows from 1 at the equator towards the poles; in the two outermost rows slot 0 reaches exactly 3 sectors ahead on even tiles and 3 sectors behind on odd tiles. slot_count grows from 1 or 2 at the equator to 8 at the two outermost rows. weights are of either sign; for each target tile the weights of each target cell over the used slots and all source cells sum (before rounding to bfloat16) to one value of that tile between 0.9 and 1.05.
All inputs are finite; a program needn't handle non-finite values.
Results may differ from a plain program's by a relative error of at most 0.0003.
Values may be sent and summed in bfloat16 or wider, within the bound.
A program may use at most 192 MiB of HBM per device.

v0:
```python
import math
import jax
import jax.numpy as jnp
from jax import lax
from jax.sharding import PartitionSpec as P

RLAT = 4
REACH = 3


def extended(value, sides, width):
    for axis, dim in sides:
        size, length = (lax.axis_size(axis), value.shape[dim])
        up = [(i, (i + 1) % size) for i in range(size - 1)]
        down = [(j, i) for i, j in up]
        last = lax.slice_in_dim(value, length - width, length, axis=dim)
        leading = lax.slice_in_dim(value, 0, width, axis=dim)
        before = lax.ppermute(last, axis, up)
        after = lax.ppermute(leading, axis, down)
        value = jnp.concatenate([before, value, after], axis=dim)
    return value


def shifted(value, axis, by):
    length = lax.axis_size(axis)
    return lax.ppermute(value, axis, [(i, (i + by) % length) for i in range(length)])


def latitude_area(total_rows, first_row, count_rows):
    rows_all = jnp.arange(count_rows, dtype=jnp.int32) + first_row
    angle = -0.5 * math.pi + (rows_all.astype(jnp.float32) + 0.5) * (math.pi / total_rows)
    return jnp.cos(angle)


def local(tracers, weights, source_row, source_block, slot_count):
    rows_dev, tile_width, levels, tracer_kinds = tracers.shape
    channels = levels * tracer_kinds
    lat_count = lax.axis_size("lat")
    lon_count = lax.axis_size("lon")
    lat_index = lax.axis_index("lat")
    lon_index = lax.axis_index("lon")
    field = tracers.reshape(rows_dev, tile_width, channels)
    total_rows = rows_dev * lat_count
    area = latitude_area(total_rows, lat_index * rows_dev, rows_dev)
    total_area = tile_width * lon_count * jnp.sum(latitude_area(total_rows, 0, total_rows))
    mass_old = jnp.sum(area[:, None, None] * field, axis=(0, 1))
    padded = extended(field, (("lat", 0),), RLAT)
    local_row = source_row[:, 0, :] - (lat_index * rows_dev - RLAT)
    wanted = source_block[:, 0, :]
    slots_max = source_row.shape[2]
    relative = (wanted - lon_index + REACH) % lon_count - REACH
    near_list = []
    for distance in range(-(REACH - 1), REACH):
        if distance == 0:
            near_list.append(padded)
        else:
            near_list.append(shifted(padded, "lon", -distance))
    near_stack = jnp.stack(near_list, axis=1)
    near_pick = near_stack[local_row, jnp.clip(relative + REACH - 1, 0, 2 * REACH - 2)]
    polar_slab = jnp.concatenate(
        [padded[RLAT : 2 * RLAT + 1], padded[rows_dev - 1 : rows_dev + RLAT]], axis=0
    )
    far_list = [shifted(polar_slab, "lon", -distance) for distance in (-REACH, REACH)]
    upper = (jnp.arange(rows_dev, dtype=jnp.int32) < rows_dev // 2)[:, None]
    far_row = jnp.where(upper, local_row - RLAT, local_row - (rows_dev - 1) + RLAT + 1)
    far_row = jnp.clip(far_row, 0, 2 * RLAT + 1)
    far_stack = jnp.stack(far_list, axis=1)
    far_pick = far_stack[
        jnp.clip(far_row, 0, far_stack.shape[0] - 1), (relative > 0).astype(jnp.int32)
    ]
    active = jnp.arange(slots_max, dtype=jnp.int32)[None, :] < slot_count
    is_far = jnp.abs(relative) == REACH
    picked = jnp.where(
        (active & is_far)[:, :, None, None],
        far_pick,
        jnp.where(active[:, :, None, None], near_pick, jnp.zeros((), near_pick.dtype)),
    )
    advected = jnp.einsum(
        "tkij,tkjc->tic", weights[:, 0], picked, preferred_element_type=jnp.float32
    )
    mass_new = jnp.sum(area[:, None, None] * advected, axis=(0, 1))
    summed_old, summed_new = lax.psum((mass_old, mass_new), ("lat", "lon"))
    fixed = advected + (summed_old - summed_new) / total_area
    return fixed.reshape(rows_dev, tile_width, levels, tracer_kinds)


def solution(mesh):
    return jax.shard_map(
        local,
        mesh=mesh,
        in_specs=(
            P("lat", "lon", None, None),
            P("lat", "lon", None, None, None),
            P("lat", "lon", None),
            P("lat", "lon", None),
            P("lat", "lon"),
        ),
        out_specs=P("lat", "lon", None, None),
        check_vma=False,
    )
```

profile of v0, /device:TPU:10, one launch (start us, length us, event | category | flops | bytes accessed | tf_op | source)
XLA Modules:
  0.0 299.7 jit_solution(15914645323149280018)
XLA Ops:
  0.0 0.0 copy-start
  0.0 0.0 copy-start.2
  0.0 0.0 copy-start.4
  0.0 0.0 copy-start.3
  0.0 1.2 fusion.28
  1.2 1.9 collective-permute-start.2
  3.2 3.6 %collective-permute-start.3 = (bf16[4,128,128]{1,2,0:T(8,128)(2,1)S(1)}, bf16[4,128,128]{1,2,0:T(8,128)(2,1)S(1)}, u32[]{:S(2)}, u32[]{:S(2)}) collective-permute-start(bf16[4,128,128]{1,2,0:T(8,128)(2,1)S(1)} %bitcast.72), channel_id=1, source_target_pairs={{8,0},{16,8},{24,16},{9,1},{17,9},{25,17},{10,2},{18,10},{26,18},{... | collective-permute-start | bytes 393224 | tf_op jit(solution)/shard_map/ppermute | solution.py:19
  6.8 0.7 collective-permute-done.2
  7.5 1.8 collective-permute-done.3
  9.3 3.3 %pad_maximum_fusion = bf16[72,128,128]{1,2,0:T(8,128)(2,1)} fusion(bf16[4,128,128]{1,2,0:T(8,128)(2,1)S(1)} %collective-permute-done.3, bf16[64,128,128]{1,2,0:T(8,128)(2,1)} %bitcast.64, bf16[4,128,128]{1,2,0:T(8,128)(2,1)S(1)} %collective-permute-done.2), kind=kLoop, calls=%fused_computation.13 | loop fusion | flops 2359296 | bytes 4718592 | tf_op jit(solution)/shard_map/concatenate | solution.py:20
  12.6 1.6 collective-permute-start.4
  14.2 1.5 collective-permute-start.5
  15.7 1.4 collective-permute-start.6
  17.1 0.0 copy-done
  17.1 0.1 fusion.29
  17.2 2.3 collective-permute-start.7
  19.6 0.1 collective-permute-start
  19.6 0.0 copy-done.2
  19.7 0.0 copy-done.4
  19.7 0.0 copy-done.3
  19.7 153.8 %collective-permute-done = bf16[10,128,128]{1,2,0:T(8,128)(2,1)S(1)} collective-permute-done((bf16[10,128,128]{1,2,0:T(8,128)(2,1)S(1)}, bf16[10,128,128]{1,2,0:T(8,128)(2,1)S(1)}, u32[]{:S(2)}, u32[]{:S(2)}) %collective-permute-start) | collective-permute-done | bytes 327712 | tf_op jit(solution)/shard_map/ppermute | solution.py:26
  173.5 1.3 collective-permute-start.1
  174.9 0.1 copy.11
  175.0 0.1 reshape.258
  175.1 0.1 copy.9
  175.1 0.1 reshape.252
  175.2 0.1 copy.10
  175.3 0.1 copy.8
  175.4 1.4 multiply_reduce_fusion
  176.8 0.1 reduce_sum.30
  176.9 0.6 cosine_reduce_fusion
  178.1 9.5 %collective-permute-done.1 = bf16[10,128,128]{1,2,0:T(8,128)(2,1)S(1)} collective-permute-done((bf16[10,128,128]{1,2,0:T(8,128)(2,1)S(1)}, bf16[10,128,128]{1,2,0:T(8,128)(2,1)S(1)}, u32[]{:S(2)}, u32[]{:S(2)}) %collective-permute-start.1) | collective-permute-done | bytes 327712 | tf_op jit(solution)/shard_map/ppermute | solution.py:26
  187.6 0.0 copy-start.1
  187.6 0.7 copy-done.1
  188.3 1.0 pad_maximum_fusion.1
  189.4 10.8 %gather_fusion = bf16[512,128,128]{1,2,0:T(8,128)(2,1)} fusion(bf16[10,2,128,128]{2,3,0,1:T(8,128)(2,1)S(1)} %pad_maximum_fusion.1, s32[512]{0:T(512)S(1)} %reshape.252), kind=kCustom, calls=%fused_computation | custom fusion | bytes 33558528 | tf_op jit(solution)/shard_map/gather | solution.py:68
  200.2 0.0 collective-permute-done.4
  200.2 3.3 %bitcast_dynamic-update-slice_fusion.4 = bf16[72,5,128,128]{2,3,0,1:T(8,128)(2,1)} fusion(bf16[72,128,128]{1,2,0:T(8,128)(2,1)} %collective-permute-done.4), kind=kLoop, calls=%fused_computation.18 | loop fusion | bytes 4718592
  203.5 0.0 collective-permute-done.5
  203.5 3.4 %bitcast_dynamic-update-slice_fusion.3 = bf16[72,5,128,128]{2,3,0,1:T(8,128)(2,1)} fusion(bf16[72,5,128,128]{2,3,0,1:T(8,128)(2,1)} %bitcast_dynamic-update-slice_fusion.4, bf16[72,128,128]{1,2,0:T(8,128)(2,1)} %collective-permute-done.5), kind=kLoop, calls=%fused_computation.17 | loop fusion | bytes 4718592
  206.9 1.7 bitcast_dynamic-update-slice_fusion.2
  208.6 0.0 collective-permute-done.6
  208.6 3.4 %bitcast_dynamic-update-slice_fusion.1 = bf16[72,5,128,128]{2,3,0,1:T(8,128)(2,1)} fusion(bf16[72,5,128,128]{2,3,0,1:T(8,128)(2,1)} %bitcast_dynamic-update-slice_fusion.2, bf16[72,128,128]{1,2,0:T(8,128)(2,1)} %collective-permute-done.6), kind=kLoop, calls=%fused_computation.15 | loop fusion | bytes 4718592
  212.0 0.0 collective-permute-done.7
  212.0 3.4 %bitcast_dynamic-update-slice_fusion = bf16[72,5,128,128]{2,3,0,1:T(8,128)(2,1)} fusion(bf16[72,5,128,128]{2,3,0,1:T(8,128)(2,1)} %bitcast_dynamic-update-slice_fusion.1, bf16[72,128,128]{1,2,0:T(8,128)(2,1)} %collective-permute-done.7), kind=kLoop, calls=%fused_computation.14 | loop fusion | bytes 4718592 | tf_op jit(solution)/shard_map/stack | solution.py:58
  215.4 15.2 %gather_fusion.1 = bf16[512,128,128]{1,2,0:T(8,128)(2,1)} fusion(bf16[72,5,128,128]{2,3,0,1:T(8,128)(2,1)} %bitcast_dynamic-update-slice_fusion, s32[512]{0:T(512)S(1)} %reshape.258), kind=kCustom, calls=%fused_computation.1 | custom fusion | bytes 33558528 | tf_op jit(solution)/shard_map/gather | solution.py:59
  230.5 19.4 %fusion.7 = (f32[128]{0:T(128)S(1)}, f32[64,128,128,1]{2,1,3,0:T(8,128)}) fusion(f32[64]{0:T(128)S(1)} %add_cosine_fusion, bf16[64,1,8,128,128]{4,3,2,1,0:T(8,128)(2,1)} %param.6, bf16[64,8,128,128]{2,3,1,0:T(8,128)(2,1)} %bitcast.66, bf16[64,8,128,128]{2,3,1,0:T(8,128)(2,1)} %bitcast.67, pred[64,8]{1,0:T(8,128)(4,1)S(1)} %copy.10, pred[64,8]{1,0:T(8,128)(4,1)S(1)} %copy.8), kind=kOutput, calls=%fused_computation.11 | convolution fusion | flops 2166358016 | bytes 54527744 | tf_op jit(solution)/shard_map/tkij,tkjc->tic/dot_general | solution.py:78
  250.0 44.8 %all-reduce = (f32[128]{0:T(128)S(1)}, f32[128]{0:T(128)S(1)}) all-reduce(f32[128]{0:T(128)S(1)} %reduce_sum.30, f32[128]{0:T(128)S(1)} %get-tuple-element.15), channel_id=1, replica_groups=mesh['lat'=4,'lon'=8] {'lat','lon'}, use_global_device_ids=true, to_apply=%region_1.0 | all-reduce | flops 256 | bytes 2048 | tf_op jit(solution)/shard_map/psum | solution.py:82
  294.8 4.9 %bitcast_add_fusion = f32[64,128,128]{2,1,0:T(8,128)} fusion(f32[64,128,128,1]{2,1,3,0:T(8,128)} %get-tuple-element.16, f32[128]{0:T(128)S(1)} %subtract_divide_fusion), kind=kLoop, calls=%fused_computation.9 | loop fusion | flops 1048576 | bytes 8389120 | tf_op jit(solution)/shard_map/add | solution.py:83
  (6 shorter events, 0.1 us)
Async XLA Ops:
  0.0 17.1 %copy-start = (bf16[64,128,32,4]{1,3,2,0:T(4,128)(2,1)S(1)}, bf16[64,128,32,4]{1,3,2,0:T(4,128)(2,1)}, u32[]{:S(2)}) copy-start(bf16[64,128,32,4]{1,3,2,0:T(4,128)(2,1)} %param.5) | copy-start | bytes 6291460
  0.0 19.6 %copy-start.2 = (s32[64,1,8]{0,2,1:T(8,128)S(1)}, s32[64,1,8]{0,2,1:T(8,128)}, u32[]{:S(2)}) copy-start(s32[64,1,8]{0,2,1:T(8,128)} %param.8) | copy-start | bytes 6148
  0.0 19.7 %copy-start.4 = (s32[64,1]{0,1:T(1,128)S(1)}, s32[64,1]{0,1:T(1,128)}, u32[]{:S(2)}) copy-start(s32[64,1]{0,1:T(1,128)} %param.9) | copy-start | bytes 772
  0.0 19.7 %copy-start.3 = (s32[64,1,8]{0,2,1:T(8,128)S(1)}, s32[64,1,8]{0,2,1:T(8,128)}, u32[]{:S(2)}) copy-start(s32[64,1,8]{0,2,1:T(8,128)} %param.7) | copy-start | bytes 6148
  1.2 6.3 %collective-permute-start.2 = (bf16[4,128,128]{1,2,0:T(8,128)(2,1)S(1)}, bf16[4,128,128]{1,2,0:T(8,128)(2,1)S(1)}, u32[]{:S(2)}, u32[]{:S(2)}) collective-permute-start(bf16[4,128,128]{1,2,0:T(8,128)(2,1)S(1)} %bitcast.73), channel_id=1, source_target_pairs={{0,8},{8,16},{16,24},{1,9},{9,17},{17,25},{2,10},{10,18},{18,26},{... | collective-permute-start | bytes 393224 | tf_op jit(solution)/shard_map/ppermute | solution.py:18
  3.2 6.1 %collective-permute-start.3 = (bf16[4,128,128]{1,2,0:T(8,128)(2,1)S(1)}, bf16[4,128,128]{1,2,0:T(8,128)(2,1)S(1)}, u32[]{:S(2)}, u32[]{:S(2)}) collective-permute-start(bf16[4,128,128]{1,2,0:T(8,128)(2,1)S(1)} %bitcast.72), channel_id=1, source_target_pairs={{8,0},{16,8},{24,16},{9,1},{17,9},{25,17},{10,2},{18,10},{26,18},{... | collective-permute-start | bytes 393224 | tf_op jit(solution)/shard_map/ppermute | solution.py:19
  12.6 187.6 %collective-permute-start.4 = (bf16[72,128,128]{1,2,0:T(8,128)(2,1)}, bf16[72,128,128]{1,2,0:T(8,128)(2,1)}, u32[]{:S(2)}, u32[]{:S(2)}) collective-permute-start(bf16[72,128,128]{1,2,0:T(8,128)(2,1)} %pad_maximum_fusion), channel_id=1, source_target_pairs={{0,2},{1,3},{2,4},{3,5},{4,6},{5,7},{6,0},{7,1},{8,10},{9,11},{10,... | collective-permute-start | bytes 7077896 | tf_op jit(solution)/shard_map/ppermute | solution.py:26
  14.2 189.3 %collective-permute-start.5 = (bf16[72,128,128]{1,2,0:T(8,128)(2,1)}, bf16[72,128,128]{1,2,0:T(8,128)(2,1)}, u32[]{:S(2)}, u32[]{:S(2)}) collective-permute-start(bf16[72,128,128]{1,2,0:T(8,128)(2,1)} %pad_maximum_fusion), channel_id=1, source_target_pairs={{0,1},{1,2},{2,3},{3,4},{4,5},{5,6},{6,7},{7,0},{8,9},{9,10},{10,1... | collective-permute-start | bytes 7077896 | tf_op jit(solution)/shard_map/ppermute | solution.py:26
  15.7 192.9 %collective-permute-start.6 = (bf16[72,128,128]{1,2,0:T(8,128)(2,1)}, bf16[72,128,128]{1,2,0:T(8,128)(2,1)}, u32[]{:S(2)}, u32[]{:S(2)}) collective-permute-start(bf16[72,128,128]{1,2,0:T(8,128)(2,1)} %pad_maximum_fusion), channel_id=1, source_target_pairs={{0,7},{1,0},{2,1},{3,2},{4,3},{5,4},{6,5},{7,6},{8,15},{9,8},{10,9... | collective-permute-start | bytes 7077896 | tf_op jit(solution)/shard_map/ppermute | solution.py:26
  17.2 194.7 %collective-permute-start.7 = (bf16[72,128,128]{1,2,0:T(8,128)(2,1)}, bf16[72,128,128]{1,2,0:T(8,128)(2,1)}, u32[]{:S(2)}, u32[]{:S(2)}) collective-permute-start(bf16[72,128,128]{1,2,0:T(8,128)(2,1)} %pad_maximum_fusion), channel_id=1, source_target_pairs={{0,6},{1,7},{2,0},{3,1},{4,2},{5,3},{6,4},{7,5},{8,14},{9,15},{10,... | collective-permute-start | bytes 7077896 | tf_op jit(solution)/shard_map/ppermute | solution.py:26
  19.6 154.0 %collective-permute-start = (bf16[10,128,128]{1,2,0:T(8,128)(2,1)S(1)}, bf16[10,128,128]{1,2,0:T(8,128)(2,1)S(1)}, u32[]{:S(2)}, u32[]{:S(2)}) collective-permute-start(bf16[10,128,128]{1,2,0:T(8,128)(2,1)S(1)} %pad_maximum_fusion.2), channel_id=1, source_target_pairs={{0,3},{1,4},{2,5},{3,6},{4,7},{5,0},{6,1},{7,2},{8,11},{9,12},{10,... | collective-permute-start | bytes 983048 | tf_op jit(solution)/shard_map/ppermute | solution.py:26
  173.5 14.1 %collective-permute-start.1 = (bf16[10,128,128]{1,2,0:T(8,128)(2,1)S(1)}, bf16[10,128,128]{1,2,0:T(8,128)(2,1)S(1)}, u32[]{:S(2)}, u32[]{:S(2)}) collective-permute-start(bf16[10,128,128]{1,2,0:T(8,128)(2,1)S(1)} %pad_maximum_fusion.2), channel_id=1, source_target_pairs={{0,5},{1,6},{2,7},{3,0},{4,1},{5,2},{6,3},{7,4},{8,13},{9,14},{10,... | collective-permute-start | bytes 983048 | tf_op jit(solution)/shard_map/ppermute | solution.py:26
  187.6 0.7 copy-start.1
where the time goes:
time: 300 us
  waiting for transfers between devices  166 us (55%)
  blocking collectives  44.8 us (15%)
  local copies, waits for them, and re-layouts  42.2 us (14%)
  matrix products  19.4 us (6%)
  starting transfers between devices  13.7 us (5%)
  other arithmetic  13.1 us (4%)
    ppermute x6, waiting for transfers between devices, shifted(): lax.ppermute(value, axis, [(i, (i + by) % length) for i in range(length)])  163 us
    psum x1, blocking collectives, local(): summed_old, summed_new = lax.psum((mass_old, mass_new), ('lat', 'lon'))  44.8 us
    dot_general x1, matrix products, local(): jnp.einsum('tkij,tkjc->tic', weights[:, 0], picked, preferred_element_typ...  19.4 us
    gather x1, local copies, waits for them, and re-layouts, local(): near_stack[local_row, jnp.clip(relative + REACH - 1, 0, 2 * REACH - 2)]  15.2 us
    unnamed x13, local copies, waits for them, and re-layouts  10.8 us
    gather x1, local copies, waits for them, and re-layouts, local(): far_stack[jnp.clip(far_row, 0, far_stack.shape[0] - 1), (relative > 0).as...  10.8 us
    ppermute x6, starting transfers between devices, shifted(): lax.ppermute(value, axis, [(i, (i + by) % length) for i in range(length)])  8.16 us
  transfers between devices with their start and end apart: 8, of which 4 were waited for; matrix products, arithmetic and copies ran while one was open for 9% of the time, Pallas kernels for 0%

commit v1 on v0

--- a/solution.py
+++ b/solution.py
@@ -79,7 +79,7 @@
         "tkij,tkjc->tic", weights[:, 0], picked, preferred_element_type=jnp.float32
     )
     mass_new = jnp.sum(area[:, None, None] * advected, axis=(0, 1))
-    summed_old, summed_new = lax.psum((mass_old, mass_new), ("lat", "lon"))
+    summed_old, summed_new = lax.psum(lax.psum((mass_old, mass_new), "lon"), "lat")
     fixed = advected + (summed_old - summed_new) / total_area
     return fixed.reshape(rows_dev, tile_width, levels, tracer_kinds)
 

time: 300 us -> 286 us (0.953)
  the two profiles are of different devices: /device:TPU:10 before, /device:TPU:0 now
where the time goes in v1:
time: 286 us; the launch traced here: 285 us
  waiting for transfers between devices  176 us (62%)
  local copies, waits for them, and re-layouts  42.2 us (15%)
  blocking collectives  22.9 us (8%)
  matrix products  19.4 us (7%)
  other arithmetic  13.1 us (5%)
  starting transfers between devices  10.6 us (4%)
    ppermute x6, waiting for transfers between devices, shifted(): lax.ppermute(value, axis, [(i, (i + by) % length) for i in range(length)])  172 us
    dot_general x1, matrix products, local(): jnp.einsum('tkij,tkjc->tic', weights[:, 0], picked, preferred_element_typ...  19.4 us
    psum x1, blocking collectives, local(): lax.psum((mass_old, mass_new), 'lon')  17.1 us
    gather x1, local copies, waits for them, and re-layouts, local(): near_stack[local_row, jnp.clip(relative + REACH - 1, 0, 2 * REACH - 2)]  15.2 us
    unnamed x13, local copies, waits for them, and re-layouts  10.8 us
    gather x1, local copies, waits for them, and re-layouts, local(): far_stack[jnp.clip(far_row, 0, far_stack.shape[0] - 1), (relative > 0).as...  10.8 us
    ppermute x6, starting transfers between devices, shifted(): lax.ppermute(value, axis, [(i, (i + by) % length) for i in range(length)])  6.86 us
    psum x1, blocking collectives, local(): lax.psum(lax.psum((mass_old, mass_new), 'lon'), 'lat')  5.74 us
  transfers between devices with their start and end apart: 8, of which 3 were waited for; matrix products, arithmetic and copies ran while one was open for 9% of the time, Pallas kernels for 0%

profile of v1, /device:TPU:0, one launch (start us, length us, event | category | flops | bytes accessed | tf_op | source)
XLA Modules:
  0.0 285.1 jit_solution(1484090268252561327)
XLA Ops:
  0.0 0.0 copy-start
  0.0 0.0 copy-start.2
  0.0 0.0 copy-start.4
  0.0 0.0 copy-start.3
  0.0 1.2 fusion.28
  1.2 2.4 collective-permute-start.2
  3.6 1.3 collective-permute-start.3
  4.9 0.0 collective-permute-done.2
  5.0 4.0 %collective-permute-done.3 = bf16[4,128,128]{1,2,0:T(8,128)(2,1)S(1)} collective-permute-done((bf16[4,128,128]{1,2,0:T(8,128)(2,1)S(1)}, bf16[4,128,128]{1,2,0:T(8,128)(2,1)S(1)}, u32[]{:S(2)}, u32[]{:S(2)}) %collective-permute-start.3) | collective-permute-done | bytes 131104 | tf_op jit(solution)/shard_map/ppermute | solution.py:19
  9.0 3.3 %pad_maximum_fusion = bf16[72,128,128]{1,2,0:T(8,128)(2,1)} fusion(bf16[4,128,128]{1,2,0:T(8,128)(2,1)S(1)} %collective-permute-done.3, bf16[64,128,128]{1,2,0:T(8,128)(2,1)} %bitcast.64, bf16[4,128,128]{1,2,0:T(8,128)(2,1)S(1)} %collective-permute-done.2), kind=kLoop, calls=%fused_computation.13 | loop fusion | flops 2359296 | bytes 4718592 | tf_op jit(solution)/shard_map/concatenate | solution.py:20
  12.3 1.6 collective-permute-start.4
  13.8 1.5 collective-permute-start.5
  15.4 3.2 %collective-permute-start.6 = (bf16[72,128,128]{1,2,0:T(8,128)(2,1)}, bf16[72,128,128]{1,2,0:T(8,128)(2,1)}, u32[]{:S(2)}, u32[]{:S(2)}) collective-permute-start(bf16[72,128,128]{1,2,0:T(8,128)(2,1)} %pad_maximum_fusion), channel_id=1, source_target_pairs={{0,7},{1,0},{2,1},{3,2},{4,3},{5,4},{6,5},{7,6},{8,15},{9,8},{10,9... | collective-permute-start | bytes 7077896 | tf_op jit(solution)/shard_map/ppermute | solution.py:26
  18.6 0.0 copy-done
  18.6 0.1 fusion.29
  18.7 0.5 collective-permute-start.7
  19.2 0.1 collective-permute-start
  19.3 0.0 copy-done.2
  19.3 0.0 copy-done.4
  19.4 0.0 copy-done.3
  19.4 165.0 %collective-permute-done = bf16[10,128,128]{1,2,0:T(8,128)(2,1)S(1)} collective-permute-done((bf16[10,128,128]{1,2,0:T(8,128)(2,1)S(1)}, bf16[10,128,128]{1,2,0:T(8,128)(2,1)S(1)}, u32[]{:S(2)}, u32[]{:S(2)}) %collective-permute-start) | collective-permute-done | bytes 327712 | tf_op jit(solution)/shard_map/ppermute | solution.py:26
  184.4 0.0 collective-permute-start.1
  184.5 0.1 copy.11
  184.6 0.1 reshape.258
  184.6 0.1 copy.9
  184.7 0.1 reshape.252
  184.8 0.1 copy.10
  184.9 0.1 copy.8
  185.0 1.4 multiply_reduce_fusion
  186.4 0.1 reduce_sum.30
  186.5 0.6 cosine_reduce_fusion
  187.7 7.3 %collective-permute-done.1 = bf16[10,128,128]{1,2,0:T(8,128)(2,1)S(1)} collective-permute-done((bf16[10,128,128]{1,2,0:T(8,128)(2,1)S(1)}, bf16[10,128,128]{1,2,0:T(8,128)(2,1)S(1)}, u32[]{:S(2)}, u32[]{:S(2)}) %collective-permute-start.1) | collective-permute-done | bytes 327712 | tf_op jit(solution)/shard_map/ppermute | solution.py:26
  195.0 0.0 copy-start.1
  195.1 0.7 copy-done.1
  195.8 1.0 pad_maximum_fusion.1
  196.8 10.8 %gather_fusion = bf16[512,128,128]{1,2,0:T(8,128)(2,1)} fusion(bf16[10,2,128,128]{2,3,0,1:T(8,128)(2,1)S(1)} %pad_maximum_fusion.1, s32[512]{0:T(512)S(1)} %reshape.252), kind=kCustom, calls=%fused_computation | custom fusion | bytes 33558528 | tf_op jit(solution)/shard_map/gather | solution.py:68
  207.6 0.0 collective-permute-done.4
  207.6 3.3 %bitcast_dynamic-update-slice_fusion.4 = bf16[72,5,128,128]{2,3,0,1:T(8,128)(2,1)} fusion(bf16[72,128,128]{1,2,0:T(8,128)(2,1)} %collective-permute-done.4), kind=kLoop, calls=%fused_computation.18 | loop fusion | bytes 4718592
  210.9 0.0 collective-permute-done.5
  210.9 3.4 %bitcast_dynamic-update-slice_fusion.3 = bf16[72,5,128,128]{2,3,0,1:T(8,128)(2,1)} fusion(bf16[72,5,128,128]{2,3,0,1:T(8,128)(2,1)} %bitcast_dynamic-update-slice_fusion.4, bf16[72,128,128]{1,2,0:T(8,128)(2,1)} %collective-permute-done.5), kind=kLoop, calls=%fused_computation.17 | loop fusion | bytes 4718592
  214.3 1.7 bitcast_dynamic-update-slice_fusion.2
  216.0 0.0 collective-permute-done.6
  216.0 3.4 %bitcast_dynamic-update-slice_fusion.1 = bf16[72,5,128,128]{2,3,0,1:T(8,128)(2,1)} fusion(bf16[72,5,128,128]{2,3,0,1:T(8,128)(2,1)} %bitcast_dynamic-update-slice_fusion.2, bf16[72,128,128]{1,2,0:T(8,128)(2,1)} %collective-permute-done.6), kind=kLoop, calls=%fused_computation.15 | loop fusion | bytes 4718592
  219.4 0.0 collective-permute-done.7
  219.4 3.4 %bitcast_dynamic-update-slice_fusion = bf16[72,5,128,128]{2,3,0,1:T(8,128)(2,1)} fusion(bf16[72,5,128,128]{2,3,0,1:T(8,128)(2,1)} %bitcast_dynamic-update-slice_fusion.1, bf16[72,128,128]{1,2,0:T(8,128)(2,1)} %collective-permute-done.7), kind=kLoop, calls=%fused_computation.14 | loop fusion | bytes 4718592 | tf_op jit(solution)/shard_map/stack | solution.py:58
  222.8 15.2 %gather_fusion.1 = bf16[512,128,128]{1,2,0:T(8,128)(2,1)} fusion(bf16[72,5,128,128]{2,3,0,1:T(8,128)(2,1)} %bitcast_dynamic-update-slice_fusion, s32[512]{0:T(512)S(1)} %reshape.258), kind=kCustom, calls=%fused_computation.1 | custom fusion | bytes 33558528 | tf_op jit(solution)/shard_map/gather | solution.py:59
  237.9 19.4 %fusion.7 = (f32[128]{0:T(128)S(1)}, f32[64,128,128,1]{2,1,3,0:T(8,128)}) fusion(f32[64]{0:T(128)S(1)} %add_cosine_fusion, bf16[64,1,8,128,128]{4,3,2,1,0:T(8,128)(2,1)} %param.6, bf16[64,8,128,128]{2,3,1,0:T(8,128)(2,1)} %bitcast.66, bf16[64,8,128,128]{2,3,1,0:T(8,128)(2,1)} %bitcast.67, pred[64,8]{1,0:T(8,128)(4,1)S(1)} %copy.10, pred[64,8]{1,0:T(8,128)(4,1)S(1)} %copy.8), kind=kOutput, calls=%fused_computation.11 | convolution fusion | flops 2166358016 | bytes 54527744 | tf_op jit(solution)/shard_map/tkij,tkjc->tic/dot_general | solution.py:78
  257.4 17.1 %all-reduce = (f32[128]{0:T(128)S(1)}, f32[128]{0:T(128)S(1)}) all-reduce(f32[128]{0:T(128)S(1)} %reduce_sum.30, f32[128]{0:T(128)S(1)} %get-tuple-element.17), channel_id=1, replica_groups=mesh['lat'=4,'lon'=8] {'lon'}, use_global_device_ids=true, to_apply=%region_1.0 | all-reduce | flops 256 | bytes 2048 | tf_op jit(solution)/shard_map/psum | solution.py:82
  274.5 5.7 %all-reduce.1 = (f32[128]{0:T(128)S(1)}, f32[128]{0:T(128)S(1)}) all-reduce(f32[128]{0:T(128)S(1)} %get-tuple-element.5, f32[128]{0:T(128)S(1)} %get-tuple-element.6), channel_id=1, replica_groups=mesh['lat'=4,'lon'=8] {'lat'}, use_global_device_ids=true, to_apply=%region_2.3 | all-reduce | flops 256 | bytes 2048 | tf_op jit(solution)/shard_map/psum | solution.py:82
  280.2 4.9 %bitcast_add_fusion = f32[64,128,128]{2,1,0:T(8,128)} fusion(f32[64,128,128,1]{2,1,3,0:T(8,128)} %get-tuple-element.18, f32[128]{0:T(128)S(1)} %subtract_divide_fusion), kind=kLoop, calls=%fused_computation.9 | loop fusion | flops 1048576 | bytes 8389120 | tf_op jit(solution)/shard_map/add | solution.py:83
  (6 shorter events, 0.1 us)
Async XLA Ops:
  0.0 18.6 %copy-start = (bf16[64,128,32,4]{1,3,2,0:T(4,128)(2,1)S(1)}, bf16[64,128,32,4]{1,3,2,0:T(4,128)(2,1)}, u32[]{:S(2)}) copy-start(bf16[64,128,32,4]{1,3,2,0:T(4,128)(2,1)} %param.5) | copy-start | bytes 6291460
  0.0 19.3 %copy-start.2 = (s32[64,1,8]{0,2,1:T(8,128)S(1)}, s32[64,1,8]{0,2,1:T(8,128)}, u32[]{:S(2)}) copy-start(s32[64,1,8]{0,2,1:T(8,128)} %param.8) | copy-start | bytes 6148
  0.0 19.3 %copy-start.4 = (s32[64,1]{0,1:T(1,128)S(1)}, s32[64,1]{0,1:T(1,128)}, u32[]{:S(2)}) copy-start(s32[64,1]{0,1:T(1,128)} %param.9) | copy-start | bytes 772
  0.0 19.4 %copy-start.3 = (s32[64,1,8]{0,2,1:T(8,128)S(1)}, s32[64,1,8]{0,2,1:T(8,128)}, u32[]{:S(2)}) copy-start(s32[64,1,8]{0,2,1:T(8,128)} %param.7) | copy-start | bytes 6148
  1.2 3.7 %collective-permute-start.2 = (bf16[4,128,128]{1,2,0:T(8,128)(2,1)S(1)}, bf16[4,128,128]{1,2,0:T(8,128)(2,1)S(1)}, u32[]{:S(2)}, u32[]{:S(2)}) collective-permute-start(bf16[4,128,128]{1,2,0:T(8,128)(2,1)S(1)} %bitcast.73), channel_id=1, source_target_pairs={{0,8},{8,16},{16,24},{1,9},{9,17},{17,25},{2,10},{10,18},{18,26},{... | collective-permute-start | bytes 393224 | tf_op jit(solution)/shard_map/ppermute | solution.py:18
  3.6 5.3 %collective-permute-start.3 = (bf16[4,128,128]{1,2,0:T(8,128)(2,1)S(1)}, bf16[4,128,128]{1,2,0:T(8,128)(2,1)S(1)}, u32[]{:S(2)}, u32[]{:S(2)}) collective-permute-start(bf16[4,128,128]{1,2,0:T(8,128)(2,1)S(1)} %bitcast.72), channel_id=1, source_target_pairs={{8,0},{16,8},{24,16},{9,1},{17,9},{25,17},{10,2},{18,10},{26,18},{... | collective-permute-start | bytes 393224 | tf_op jit(solution)/shard_map/ppermute | solution.py:19
  12.3 195.3 %collective-permute-start.4 = (bf16[72,128,128]{1,2,0:T(8,128)(2,1)}, bf16[72,128,128]{1,2,0:T(8,128)(2,1)}, u32[]{:S(2)}, u32[]{:S(2)}) collective-permute-start(bf16[72,128,128]{1,2,0:T(8,128)(2,1)} %pad_maximum_fusion), channel_id=1, source_target_pairs={{0,2},{1,3},{2,4},{3,5},{4,6},{5,7},{6,0},{7,1},{8,10},{9,11},{10,... | collective-permute-start | bytes 7077896 | tf_op jit(solution)/shard_map/ppermute | solution.py:26
  13.8 197.1 %collective-permute-start.5 = (bf16[72,128,128]{1,2,0:T(8,128)(2,1)}, bf16[72,128,128]{1,2,0:T(8,128)(2,1)}, u32[]{:S(2)}, u32[]{:S(2)}) collective-permute-start(bf16[72,128,128]{1,2,0:T(8,128)(2,1)} %pad_maximum_fusion), channel_id=1, source_target_pairs={{0,1},{1,2},{2,3},{3,4},{4,5},{5,6},{6,7},{7,0},{8,9},{9,10},{10,1... | collective-permute-start | bytes 7077896 | tf_op jit(solution)/shard_map/ppermute | solution.py:26
  15.4 200.7 %collective-permute-start.6 = (bf16[72,128,128]{1,2,0:T(8,128)(2,1)}, bf16[72,128,128]{1,2,0:T(8,128)(2,1)}, u32[]{:S(2)}, u32[]{:S(2)}) collective-permute-start(bf16[72,128,128]{1,2,0:T(8,128)(2,1)} %pad_maximum_fusion), channel_id=1, source_target_pairs={{0,7},{1,0},{2,1},{3,2},{4,3},{5,4},{6,5},{7,6},{8,15},{9,8},{10,9... | collective-permute-start | bytes 7077896 | tf_op jit(solution)/shard_map/ppermute | solution.py:26
  18.7 200.7 %collective-permute-start.7 = (bf16[72,128,128]{1,2,0:T(8,128)(2,1)}, bf16[72,128,128]{1,2,0:T(8,128)(2,1)}, u32[]{:S(2)}, u32[]{:S(2)}) collective-permute-start(bf16[72,128,128]{1,2,0:T(8,128)(2,1)} %pad_maximum_fusion), channel_id=1, source_target_pairs={{0,6},{1,7},{2,0},{3,1},{4,2},{5,3},{6,4},{7,5},{8,14},{9,15},{10,... | collective-permute-start | bytes 7077896 | tf_op jit(solution)/shard_map/ppermute | solution.py:26
  19.2 165.2 %collective-permute-start = (bf16[10,128,128]{1,2,0:T(8,128)(2,1)S(1)}, bf16[10,128,128]{1,2,0:T(8,128)(2,1)S(1)}, u32[]{:S(2)}, u32[]{:S(2)}) collective-permute-start(bf16[10,128,128]{1,2,0:T(8,128)(2,1)S(1)} %pad_maximum_fusion.2), channel_id=1, source_target_pairs={{0,3},{1,4},{2,5},{3,6},{4,7},{5,0},{6,1},{7,2},{8,11},{9,12},{10,... | collective-permute-start | bytes 983048 | tf_op jit(solution)/shard_map/ppermute | solution.py:26
  184.4 10.6 %collective-permute-start.1 = (bf16[10,128,128]{1,2,0:T(8,128)(2,1)S(1)}, bf16[10,128,128]{1,2,0:T(8,128)(2,1)S(1)}, u32[]{:S(2)}, u32[]{:S(2)}) collective-permute-start(bf16[10,128,128]{1,2,0:T(8,128)(2,1)S(1)} %pad_maximum_fusion.2), channel_id=1, source_target_pairs={{0,5},{1,6},{2,7},{3,0},{4,1},{5,2},{6,3},{7,4},{8,13},{9,14},{10,... | collective-permute-start | bytes 983048 | tf_op jit(solution)/shard_map/ppermute | solution.py:26
  195.0 0.7 copy-start.1
